TPU v7x, 32 devices: a whole 2x2x4 slice. The times are simulated.
32 devices in a mesh: wide: 8 (over z, y), narrow: 4 (over x, core).
Axes of the slice: x: 2, y: 2, z: 4, core: 2. Of those that a mesh axis runs over, the one named last changes fastest.
Arguments:
- tokens: bfloat16 [32768, 768], P(('wide', 'narrow')), may hold values from -6 to 6
- lengths: int32 [32], P(('wide', 'narrow')), may hold values from 512 to 1024, as said below
- query_weight: bfloat16 [768, 768], P(('wide', 'narrow')), may hold values from -0.25 to 0.25
- key_weight: bfloat16 [768, 768], P(('wide', 'narrow')), may hold values from -0.25 to 0.25
- value_weight: bfloat16 [768, 768], P(('wide', 'narrow')), may hold values from -0.21875 to 0.21875
- query_bias: bfloat16 [768], P(('wide', 'narrow')), may hold values from -3 to 3
- value_bias: bfloat16 [768], P(('wide', 'narrow')), may hold values from -3 to 3
- conv_weight: bfloat16 [12, 33], replicated, may hold values from -0.29882812 to 0.29882812
- output_weight: bfloat16 [768, 768], P(('wide', 'narrow')), may hold values from -0.875 to 0.875
- output_bias: bfloat16 [768], P(('wide', 'narrow')), may hold values from -3 to 3
- norm_gain: bfloat16 [768], P(('wide', 'narrow')), may hold values from 0.5 to 1.5
- norm_bias: bfloat16 [768], P(('wide', 'narrow')), may hold values from -1.796875 to 1.796875
- up_weight: bfloat16 [768, 3072], P(('wide', 'narrow')), may hold values from -0.21875 to 0.21875
- up_bias: bfloat16 [3072], P(('wide', 'narrow')), may hold values from -3 to 3
- down_weight: bfloat16 [3072, 768], P(('wide', 'narrow')), may hold values from -0.109375 to 0.109375
- down_bias: bfloat16 [768], P(('wide', 'narrow')), may hold values from -1.796875 to 1.796875
- final_gain: bfloat16 [768], P(('wide', 'narrow')), may hold values from 0.5 to 1.5
- final_bias: bfloat16 [768], P(('wide', 'narrow')), may hold values from -1.796875 to 1.796875
- cotangent: bfloat16 [32768, 768], P(('wide', 'narrow')), may hold values from -6 to 6
Outputs:
- result: float32 [32768, 768], P(('wide', 'narrow'))
- tokens_grad: float32 [32768, 768], P(('wide', 'narrow'))
- query_weight_grad: float32 [768, 768], P(('wide', 'narrow'))
- key_weight_grad: float32 [768, 768], P(('wide', 'narrow'))
- value_weight_grad: float32 [768, 768], P(('wide', 'narrow'))
- query_bias_grad: float32 [768], P(('wide', 'narrow'))
- value_bias_grad: float32 [768], P(('wide', 'narrow'))
- conv_weight_grad: float32 [12, 33], replicated
- output_weight_grad: float32 [768, 768], P(('wide', 'narrow'))
- output_bias_grad: float32 [768], P(('wide', 'narrow'))
- norm_gain_grad: float32 [768], P(('wide', 'narrow'))
- norm_bias_grad: float32 [768], P(('wide', 'narrow'))
- up_weight_grad: float32 [768, 3072], P(('wide', 'narrow'))
- up_bias_grad: float32 [3072], P(('wide', 'narrow'))
- down_weight_grad: float32 [3072, 768], P(('wide', 'narrow'))
- down_bias_grad: float32 [768], P(('wide', 'narrow'))
- final_gain_grad: float32 [768], P(('wide', 'narrow'))
- final_bias_grad: float32 [768], P(('wide', 'narrow'))
- proxy: float32 [12], replicated
Inputs may be any that keep to these rules, and one draw needn't show every extreme that they name: `lengths`: each sequence's true length; its positions from that length on are padding.
All inputs are finite; a program needn't handle non-finite values.
Results may differ from a plain program's by a relative error of at most 0.009.
Values may be sent and summed in bfloat16 or wider, within the bound.
A program may use at most 320 MiB of HBM per device.

v0:
```python
import jax
import jax.numpy as jnp
from jax import lax
from jax.sharding import PartitionSpec as P

MARKS = 64
NEWTON = 6


EPSILON = 1e-05
MASKED_SCORE = 1000000000.0


def batch_mapped(form, left, right):
    return jnp.einsum(
        form, left, right, precision=lax.Precision.HIGHEST, preferred_element_type=jnp.float32
    )


def matmul(left, right):
    return jnp.dot(left, right, preferred_element_type=jnp.float32)


def matmul_left_t(left, right):
    return lax.dot_general(
        left, right, (((0,), (0,)), ((), ())), preferred_element_type=jnp.float32
    )


def matmul_right_t(left, right):
    return lax.dot_general(
        left, right, (((1,), (1,)), ((), ())), preferred_element_type=jnp.float32
    )


def softmax_final_axis(scores):
    top = jnp.max(scores, axis=-1, keepdims=True)
    powers = jnp.exp(scores - top)
    return powers / jnp.sum(powers, axis=-1, keepdims=True)


def newton_inverse(kernel):
    marks = kernel.shape[-1]
    identity = jnp.eye(marks, dtype=jnp.float32)
    column_max = jnp.max(jnp.sum(kernel, axis=-2), axis=-1)
    pseudo_inverse = jnp.swapaxes(kernel, -1, -2) / column_max[:, None, None]
    for sweep in range(NEWTON):
        product = batch_mapped("hmn,hnp->hmp", kernel, pseudo_inverse)
        inner = 7.0 * identity - product
        inner = 15.0 * identity - batch_mapped("hmn,hnp->hmp", product, inner)
        inner = 13.0 * identity - batch_mapped("hmn,hnp->hmp", product, inner)
        pseudo_inverse = 0.25 * batch_mapped("hmn,hnp->hmp", pseudo_inverse, inner)
    return pseudo_inverse


def attention_core(queries, keys, values, conv_weight, length):
    seq_len = queries.shape[0]
    heads = conv_weight.shape[0]
    width = conv_weight.shape[1]
    head_dim = queries.shape[1] // heads
    scale = head_dim ** (-0.25)
    marks = MARKS
    position = jnp.arange(seq_len, dtype=jnp.int32)
    valid_mask = (position < length).astype(jnp.float32)
    marker = jnp.arange(marks, dtype=jnp.int32)
    lower = marker * length // marks
    upper = (marker + 1) * length // marks
    inside = jnp.logical_and(
        position[None, :] >= lower[:, None], position[None, :] < upper[:, None]
    )
    counts = (upper - lower).astype(jnp.float32)
    segment_averager = inside.astype(jnp.float32) / counts[:, None]
    query_per_head = (queries * scale).reshape(seq_len, heads, head_dim)
    key_per_head = (keys * scale).reshape(seq_len, heads, head_dim)
    value_per_head = (values * valid_mask[:, None]).reshape(seq_len, heads, head_dim)
    query_landmarks = batch_mapped("vi,iqj->qvj", segment_averager, query_per_head)
    key_landmarks = batch_mapped("vi,iqj->qvj", segment_averager, key_per_head)
    first_kernel = softmax_final_axis(batch_mapped("bsz,scz->sbc", query_per_head, key_landmarks))
    second_kernel = softmax_final_axis(batch_mapped("pus,pos->puo", query_landmarks, key_landmarks))
    third_score_matrix = (
        batch_mapped("ncf,xnf->ncx", query_landmarks, key_per_head)
        + (valid_mask - 1.0) * MASKED_SCORE
    )
    third_kernel = softmax_final_axis(third_score_matrix)
    landmark_value_rows = batch_mapped("iob,bia->ioa", third_kernel, value_per_head)
    pseudo_inverse = newton_inverse(second_kernel)
    mixed_output = batch_mapped("xkc,xcl->xkl", pseudo_inverse, landmark_value_rows)
    nystrom_attention = batch_mapped("bqj,bjg->qbg", first_kernel, mixed_output)
    half = (width - 1) // 2
    padded = jnp.pad(value_per_head, ((half, half), (0, 0), (0, 0)))
    convolved = jnp.zeros_like(value_per_head)
    for offset in range(width):
        convolved = (
            convolved + conv_weight[:, offset][None, :, None] * padded[offset : offset + seq_len]
        )
    context = ((nystrom_attention + convolved) * valid_mask[:, None, None]).reshape(
        seq_len, heads * head_dim
    )
    proxy = (
        jnp.sqrt(jnp.sum(second_kernel * second_kernel, axis=(1, 2)))
        * jnp.sqrt(jnp.sum(pseudo_inverse * pseudo_inverse, axis=(1, 2)))
        / marks
    )
    return (context, proxy)


def layer_norm(rows, gain, shift):
    centered = rows - jnp.mean(rows, axis=-1, keepdims=True)
    variance = jnp.mean(centered * centered, axis=-1, keepdims=True)
    return centered * lax.rsqrt(variance + EPSILON) * gain + shift


def gelu_exact(values):
    return 0.5 * values * (1.0 + jax.scipy.special.erf(values * 0.5**0.5))


def column_sums(rows):
    return jnp.sum(rows.astype(jnp.float32), axis=0)


def on_device(
    tokens,
    lengths,
    query_weight,
    key_weight,
    value_weight,
    query_bias,
    value_bias,
    conv_weight,
    output_weight,
    output_bias,
    norm_gain,
    norm_bias,
    up_weight,
    up_bias,
    down_weight,
    down_bias,
    final_gain,
    final_bias,
    cotangent,
):
    seq_count = lengths.shape[0]
    seq_len = tokens.shape[0] // seq_count
    width = tokens.shape[1]
    devices = lax.axis_size(("wide", "narrow"))
    shaped = (seq_count, seq_len, width)
    attention_full = (
        lax.all_gather(query_weight, ("wide", "narrow"), axis=0, tiled=True),
        lax.all_gather(key_weight, ("wide", "narrow"), axis=0, tiled=True),
        lax.all_gather(value_weight, ("wide", "narrow"), axis=0, tiled=True),
        lax.all_gather(output_weight, ("wide", "narrow"), axis=0, tiled=True),
        lax.all_gather(query_bias, ("wide", "narrow"), axis=0, tiled=True),
        lax.all_gather(value_bias, ("wide", "narrow"), axis=0, tiled=True),
        lax.all_gather(output_bias, ("wide", "narrow"), axis=0, tiled=True),
        lax.all_gather(norm_gain, ("wide", "narrow"), axis=0, tiled=True),
        lax.all_gather(norm_bias, ("wide", "narrow"), axis=0, tiled=True),
    )
    (
        query_full,
        key_full,
        value_full,
        output_full,
        query_add,
        value_add,
        output_add,
        gain_one,
        shift_one,
    ) = attention_full
    queries = matmul(tokens, query_full) + query_add.astype(jnp.float32)
    keys = matmul(tokens, key_full)
    values = matmul(tokens, value_full) + value_add.astype(jnp.float32)
    conv_float = conv_weight.astype(jnp.float32)

    def core_batch(query_in, key_in, value_in, conv_in):
        return jax.vmap(attention_core, in_axes=(0, 0, 0, None, 0))(
            query_in, key_in, value_in, conv_in, lengths
        )

    context, core_back, proxies = jax.vjp(
        core_batch,
        queries.reshape(shaped),
        keys.reshape(shaped),
        values.reshape(shaped),
        conv_float,
        has_aux=True,
    )
    context_low = context.reshape(tokens.shape).astype(jnp.bfloat16)
    first_sum = (
        tokens.astype(jnp.float32)
        + matmul(context_low, output_full)
        + output_add.astype(jnp.float32)
    )
    first_norm, norm_back = jax.vjp(
        layer_norm, first_sum, gain_one.astype(jnp.float32), shift_one.astype(jnp.float32)
    )
    hidden_low = first_norm.astype(jnp.bfloat16)
    feed_full = (
        lax.all_gather(up_weight, ("wide", "narrow"), axis=0, tiled=True),
        lax.all_gather(down_weight, ("wide", "narrow"), axis=0, tiled=True),
        lax.all_gather(up_bias, ("wide", "narrow"), axis=0, tiled=True),
        lax.all_gather(down_bias, ("wide", "narrow"), axis=0, tiled=True),
        lax.all_gather(final_gain, ("wide", "narrow"), axis=0, tiled=True),
        lax.all_gather(final_bias, ("wide", "narrow"), axis=0, tiled=True),
    )
    up_full, down_full, up_add, down_add, gain_two, shift_two = feed_full
    up_rows = matmul(hidden_low, up_full) + up_add.astype(jnp.float32)
    activated, gelu_back = jax.vjp(gelu_exact, up_rows)
    activated_low = activated.astype(jnp.bfloat16)
    second_sum = first_norm + matmul(activated_low, down_full) + down_add.astype(jnp.float32)
    result, final_back = jax.vjp(
        layer_norm, second_sum, gain_two.astype(jnp.float32), shift_two.astype(jnp.float32)
    )
    feed_again = (
        lax.all_gather(up_weight, ("wide", "narrow"), axis=0, tiled=True),
        lax.all_gather(down_weight, ("wide", "narrow"), axis=0, tiled=True),
        lax.all_gather(up_bias, ("wide", "narrow"), axis=0, tiled=True),
        lax.all_gather(down_bias, ("wide", "narrow"), axis=0, tiled=True),
        lax.all_gather(final_gain, ("wide", "narrow"), axis=0, tiled=True),
        lax.all_gather(final_bias, ("wide", "narrow"), axis=0, tiled=True),
    )
    up_back = feed_again[0]
    down_back = feed_again[1]
    second_grad, final_gain_grad, final_bias_grad = final_back(cotangent.astype(jnp.float32))
    down_in = second_grad.astype(jnp.bfloat16)
    down_weight_grad = matmul_left_t(activated_low, down_in)
    down_bias_grad = column_sums(down_in)
    (up_grad,) = gelu_back(matmul_right_t(down_in, down_back))
    up_in = up_grad.astype(jnp.bfloat16)
    up_weight_grad = matmul_left_t(hidden_low, up_in)
    up_bias_grad = column_sums(up_in)
    hidden_grad = second_grad + matmul_right_t(up_in, up_back)
    feed_owned = (
        lax.psum_scatter(up_weight_grad, ("wide", "narrow"), scatter_dimension=0, tiled=True),
        lax.psum_scatter(down_weight_grad, ("wide", "narrow"), scatter_dimension=0, tiled=True),
        lax.psum_scatter(up_bias_grad, ("wide", "narrow"), scatter_dimension=0, tiled=True),
        lax.psum_scatter(down_bias_grad, ("wide", "narrow"), scatter_dimension=0, tiled=True),
        lax.psum_scatter(final_gain_grad, ("wide", "narrow"), scatter_dimension=0, tiled=True),
        lax.psum_scatter(final_bias_grad, ("wide", "narrow"), scatter_dimension=0, tiled=True),
    )
    attention_again = (
        lax.all_gather(query_weight, ("wide", "narrow"), axis=0, tiled=True),
        lax.all_gather(key_weight, ("wide", "narrow"), axis=0, tiled=True),
        lax.all_gather(value_weight, ("wide", "narrow"), axis=0, tiled=True),
        lax.all_gather(output_weight, ("wide", "narrow"), axis=0, tiled=True),
        lax.all_gather(query_bias, ("wide", "narrow"), axis=0, tiled=True),
        lax.all_gather(value_bias, ("wide", "narrow"), axis=0, tiled=True),
        lax.all_gather(output_bias, ("wide", "narrow"), axis=0, tiled=True),
        lax.all_gather(norm_gain, ("wide", "narrow"), axis=0, tiled=True),
        lax.all_gather(norm_bias, ("wide", "narrow"), axis=0, tiled=True),
    )
    query_back = attention_again[0]
    key_back = attention_again[1]
    value_back = attention_again[2]
    output_back = attention_again[3]
    first_grad, norm_gain_grad, norm_bias_grad = norm_back(hidden_grad)
    attend_in = first_grad.astype(jnp.bfloat16)
    output_weight_grad = matmul_left_t(context_low, attend_in)
    output_bias_grad = column_sums(attend_in)
    context_grad = matmul_right_t(attend_in, output_back).reshape(shaped)
    query_grad, key_grad, value_grad, conv_grad = core_back(context_grad)
    query_in = query_grad.reshape(tokens.shape).astype(jnp.bfloat16)
    key_in = key_grad.reshape(tokens.shape).astype(jnp.bfloat16)
    value_in = value_grad.reshape(tokens.shape).astype(jnp.bfloat16)
    query_weight_grad = matmul_left_t(tokens, query_in)
    key_weight_grad = matmul_left_t(tokens, key_in)
    value_weight_grad = matmul_left_t(tokens, value_in)
    query_bias_grad = column_sums(query_in)
    value_bias_grad = column_sums(value_in)
    tokens_grad = (
        first_grad
        + matmul_right_t(query_in, query_back)
        + matmul_right_t(key_in, key_back)
        + matmul_right_t(value_in, value_back)
    )
    attention_owned = (
        lax.psum_scatter(query_weight_grad, ("wide", "narrow"), scatter_dimension=0, tiled=True),
        lax.psum_scatter(key_weight_grad, ("wide", "narrow"), scatter_dimension=0, tiled=True),
        lax.psum_scatter(value_weight_grad, ("wide", "narrow"), scatter_dimension=0, tiled=True),
        lax.psum_scatter(output_weight_grad, ("wide", "narrow"), scatter_dimension=0, tiled=True),
        lax.psum_scatter(query_bias_grad, ("wide", "narrow"), scatter_dimension=0, tiled=True),
        lax.psum_scatter(value_bias_grad, ("wide", "narrow"), scatter_dimension=0, tiled=True),
        lax.psum_scatter(output_bias_grad, ("wide", "narrow"), scatter_dimension=0, tiled=True),
        lax.psum_scatter(norm_gain_grad, ("wide", "narrow"), scatter_dimension=0, tiled=True),
        lax.psum_scatter(norm_bias_grad, ("wide", "narrow"), scatter_dimension=0, tiled=True),
    )
    proxy_total, conv_total = lax.psum((jnp.sum(proxies, axis=0), conv_grad), ("wide", "narrow"))
    proxy = proxy_total / (seq_count * devices)
    return (
        result,
        tokens_grad,
        attention_owned[0],
        attention_owned[1],
        attention_owned[2],
        attention_owned[4],
        attention_owned[5],
        conv_total,
        attention_owned[3],
        attention_owned[6],
        attention_owned[7],
        attention_owned[8],
        feed_owned[0],
        feed_owned[2],
        feed_owned[1],
        feed_owned[3],
        feed_owned[4],
        feed_owned[5],
        proxy,
    )


def solution(mesh):
    return jax.shard_map(
        on_device,
        mesh=mesh,
        in_specs=(
            P(("wide", "narrow"), None),
            P(("wide", "narrow")),
            P(("wide", "narrow"), None),
            P(("wide", "narrow"), None),
            P(("wide", "narrow"), None),
            P(("wide", "narrow")),
            P(("wide", "narrow")),
            P(),
            P(("wide", "narrow"), None),
            P(("wide", "narrow")),
            P(("wide", "narrow")),
            P(("wide", "narrow")),
            P(("wide", "narrow"), None),
            P(("wide", "narrow")),
            P(("wide", "narrow"), None),
            P(("wide", "narrow")),
            P(("wide", "narrow")),
            P(("wide", "narrow")),
            P(("wide", "narrow"), None),
        ),
        out_specs=(
            P(("wide", "narrow"), None),
            P(("wide", "narrow"), None),
            P(("wide", "narrow"), None),
            P(("wide", "narrow"), None),
            P(("wide", "narrow"), None),
            P(("wide", "narrow")),
            P(("wide", "narrow")),
            P(),
            P(("wide", "narrow"), None),
            P(("wide", "narrow")),
            P(("wide", "narrow")),
            P(("wide", "narrow")),
            P(("wide", "narrow"), None),
            P(("wide", "narrow")),
            P(("wide", "narrow"), None),
            P(("wide", "narrow")),
            P(("wide", "narrow")),
            P(("wide", "narrow")),
            P(),
        ),
        check_vma=False,
    )
```

profile of v0, /device:TPU:0, one launch (start us, length us, event | category | flops | bytes accessed | tf_op | source)
XLA Modules:
  0.0 1155.7 jit_solution(17454962343338376369)
XLA Ops:
  24.6 42.4 %all-reduce.86 = (bf16[768]{0:T(1024)(128)(2,1)S(1)}, bf16[768]{0:T(1024)(128)(2,1)S(1)}, bf16[768]{0:T(1024)(128)(2,1)S(1)}, bf16[768]{0:T(1024)(128)(2,1)S(1)}...) all-reduce(bf16[768]{0:T(1024)(128)(2,1)S(1)} %dynamic-update-slice, ...), channel_id=1, replica_groups=mesh['wide'=8,'narrow'=4] {'wide','narrow'}, use_global_device_ids=true, to_apply=%add.68 | all-reduce | flops 9216 | bytes 36864
  82.2 41.4 %all-gather.9.cloned.1.call-done = bf16[768,768]{1,0:T(8,128)(2,1)} async-done(((bf16[24,768]{1,0:T(8,128)(2,1)}), bf16[768,768]{1,0:T(8,128)(2,1)}) %all-gather.9.cloned.1.call-update) | async-done | bytes 1179664 | tf_op jit(solution)/shard_map/all_gather | solution.py:149
  131.2 5.3 fusion.182
  162.5 16.8 %all-gather.11.cloned.1.call-done = bf16[768,768]{1,0:T(8,128)(2,1)} async-done(((bf16[24,768]{1,0:T(8,128)(2,1)}), bf16[768,768]{1,0:T(8,128)(2,1)}) %all-gather.11.cloned.1.call-update) | async-done | bytes 1179664 | tf_op jit(solution)/shard_map/all_gather | solution.py:150
  188.7 30.0 %fusion.10 = bf16[1,1024,12,64]{1,3,2,0:T(8,128)(2,1)} fusion(f32[1,1024,12,64]{1,3,2,0:T(8,128)S(1)} %bitcast.592, f32[12,64,64]{2,1,0:T(8,128)S(1)} %fusion.185, f32[1024]{0:T(1024)S(1)} %copy-done.130, f32[12]{0:T(128)S(1)} %copy-done.205, f32[12]{0:T(128)S(1)} %copy-done.213, f32[12]{0:T(128)S(1)} %copy-done.215, f32[12]{0:T(128)S(1)} %copy-done.217, ...), kind=kOutput, calls=%fused_computation.29 | convolution fusion | flops 659030016 | bytes 8164912 | tf_op jit(solution)/shard_map/jvp(vmap(bqj,bjg->qbg))/dot_general | solution.py:15
  218.7 16.3 %all-gather.13.cloned.1.call-done = bf16[768,768]{1,0:T(8,128)(2,1)} async-done(((bf16[24,768]{1,0:T(8,128)(2,1)}), bf16[768,768]{1,0:T(8,128)(2,1)}) %all-gather.13.cloned.1.call-update) | async-done | bytes 1179664 | tf_op jit(solution)/shard_map/all_gather | solution.py:151
  243.1 57.2 %all-gather.15.cloned.1.call-done = bf16[768,3072]{1,0:T(8,128)(2,1)} async-done(((bf16[24,3072]{1,0:T(8,128)(2,1)}), bf16[768,3072]{1,0:T(8,128)(2,1)}) %all-gather.15.cloned.1.call-update) | async-done | bytes 4718608 | tf_op jit(solution)/shard_map/all_gather | solution.py:198
  300.2 12.6 %multiply_convert_fusion = (bf16[1024,3072]{1,0:T(8,128)(2,1)}, f32[1024,3072]{1,0:T(8,128)}) fusion(f32[3072]{0:T(1024)} %convert_element_type.190, bf16[768,3072]{1,0:T(8,128)(2,1)} %all-gather.15.cloned.1.call-done, f32[1024,768]{0,1:T(8,128)S(1)} %get-tuple-element.260, f32[768]{0:T(1024)} %convert_element_type.188, f32[768]{0:T(1024)} %convert_element_type.187, ...), kind=kOutput, calls=%fused_computation.2 | convolution fusion | flops 4854644736 | bytes 26765312 | tf_op jit(solution)/shard_map/dot_general | solution.py:21
  312.8 52.1 %all-gather.17.cloned.1.call-done = bf16[3072,768]{1,0:T(8,128)(2,1)} async-done(((bf16[96,768]{1,0:T(8,128)(2,1)}), bf16[3072,768]{1,0:T(8,128)(2,1)}) %all-gather.17.cloned.1.call-update) | async-done | bytes 4718608 | tf_op jit(solution)/shard_map/all_gather | solution.py:199
  365.0 9.4 fusion.184
  382.0 15.6 %convert_reduce_fusion = (f32[3072]{0:T(1024)}, bf16[1024,3072]{1,0:T(8,128)(2,1)S(1)}) fusion(bf16[1024,768]{0,1:T(8,128)(2,1)S(1)} %get-tuple-element.192, bf16[3072,768]{1,0:T(8,128)(2,1)S(1)} %bitcast.636, f32[1024,3072]{1,0:T(8,128)} %get-tuple-element.262, f32[3072]{0:T(1024)S(1)} %copy-done.161), kind=kOutput, calls=%fused_computation | convolution fusion | flops 4882166784 | bytes 25190400 | tf_op jit(solution)/shard_map/dot_general | solution.py:31
  397.6 7.1 multiply_reduce_fusion
  498.2 6.9 fusion.17
  520.4 16.4 %broadcast_multiply_fusion.2 = (f32[1,1024,12,64]{1,3,2,0:T(8,128)}, f32[1,1024,12,64]{1,3,2,0:T(8,128)}, f32[1,1024,12,64]{1,3,2,0:T(8,128)}, f32[1,1024,12,64]...) fusion(f32[12]{0:T(128)S(1)} %copy-done.214, ...), kind=kLoop, calls=%fused_computation.153 | loop fusion | flops 13369344 | bytes 53482240 | tf_op jit(solution)/shard_map/transpose(jvp(vmap()))/mul | solution.py:94
  537.0 17.3 %broadcast_multiply_fusion.1 = (f32[1,1024,12,64]{1,3,2,0:T(8,128)}, f32[1,1024,12,64]{1,3,2,0:T(8,128)}, f32[1,1024,12,64]{1,3,2,0:T(8,128)}, f32[1,1024,12,64]...) fusion(f32[12]{0:T(128)S(1)} %copy-done.206, ...), kind=kLoop, calls=%fused_computation.152 | loop fusion | flops 14155776 | bytes 56628016 | tf_op jit(solution)/shard_map/transpose(jvp(vmap()))/mul | solution.py:94
  554.5 35.0 %pad_add_fusion = f32[1,1056,12,64]{1,3,2,0:T(8,128)} fusion(f32[1,1024,12,64]{1,3,2,0:T(8,128)} %get-tuple-element.220, f32[1,1024,12,64]{1,3,2,0:T(8,128)} %get-tuple-element.221, f32[1,1024,12,64]{1,3,2,0:T(8,128)} %get-tuple-element.222, f32[1,1024,12,64]{1,3,2,0:T(8,128)} %get-tuple-element.223, f32[1,1024,12,64]{1,3,2,0:T(8,128)} %get-tuple-element.224, ...), kind=kLoop, calls=%fused_computation.11 | loop fusion | flops 21086208 | bytes 88178688 | tf_op jit(solution)/shard_map/transpose(jvp(vmap()))/add_any | solution.py:94
  589.5 42.2 %multiply_reduce_fusion.32 = (f32[12]{0:T(128)}, f32[12]{0:T(128)}, f32[12]{0:T(128)}, f32[12]{0:T(128)}, f32[12]{0:T(128)}, /*index=5*/f32[12]{0:T(128)}, f32[1...) fusion(f32[1,1024,12,64]{1,3,2,0:T(8,128)} %bitcast.593, ...), kind=kOutput, calls=%fused_computation.70 | convolution fusion | flops 639368256 | bytes 34817744 | tf_op jit(solution)/shard_map/transpose(jvp(vmap(iob,bia->ioa)))/dot_general | solution.py:15
  642.6 10.5 fusion.151
  653.2 10.1 fusion.195
  680.8 33.2 %multiply_reduce_fusion.33 = (f32[12]{0:T(128)S(1)}, f32[12]{0:T(128)S(1)}, f32[12]{0:T(128)S(1)}, f32[12]{0:T(128)S(1)}, f32[12]{0:T(128)S(1)}, /*index=5*/f32[...) fusion(f32[1,1024,12,64]{1,3,2,0:T(8,128)} %bitcast.594, ...), kind=kLoop, calls=%fused_computation.71 | loop fusion | flops 27524916 | bytes 6296368 | tf_op jit(solution)/shard_map/transpose(jvp(vmap()))/reduce_sum | solution.py:94
  714.4 40.7 %all-reduce.85 = (f32[768]{0:T(1024)S(1)}, f32[768]{0:T(1024)S(1)}, f32[12,33]{0,1:T(8,128)S(1)}, f32[768]{0:T(1024)S(1)}, f32[768]{0:T(1024)S(1)}, /*index=5*/f...) all-reduce(f32[768]{0:T(1024)S(1)} %reduce_sum.646, ...), channel_id=5, replica_groups=mesh['wide'=8,'narrow'=4] {'wide','narrow'}, use_global_device_ids=true, to_apply=%region_31.32.clone | all-reduce | flops 9624 | bytes 76992
  761.5 104.0 %reduce-scatter.23.cloned.1.call-done = f32[24,768]{1,0:T(8,128)} async-done(((f32[768,768]{1,0:T(8,128)}), f32[24,768]{1,0:T(8,128)}) %reduce-scatter.23.cloned.1.call-update) | async-done | bytes 73744
  865.5 141.8 %reduce-scatter.15.cloned.1.call-done = f32[24,3072]{1,0:T(8,128)} async-done(((f32[768,3072]{1,0:T(8,128)}), f32[24,3072]{1,0:T(8,128)}) %reduce-scatter.15.cloned.1.call-update) | async-done | bytes 294928 | tf_op jit(solution)/shard_map/reduce_scatter | solution.py:233
  1007.3 141.4 %reduce-scatter.17.cloned.1.call-done = f32[96,768]{1,0:T(8,128)} async-done(((f32[3072,768]{1,0:T(8,128)}), f32[96,768]{1,0:T(8,128)}) %reduce-scatter.17.cloned.1.call-update) | async-done | bytes 294928 | tf_op jit(solution)/shard_map/reduce_scatter | solution.py:234
  (771 shorter events, 230.7 us)
Async XLA Ops:
  7.2 67.2 %copy-start.87 = (bf16[1024,768]{1,0:T(8,128)(2,1)S(1)}, bf16[1024,768]{1,0:T(8,128)(2,1)}, u32[]{:S(2)}) copy-start(bf16[1024,768]{1,0:T(8,128)(2,1)} %param.19) | copy-start | bytes 4718596
  7.2 69.1 %all-gather.7.cloned.1.call-start = ((), (), s32[]{:S(2)}) async-start(), calls=%async_computation.6 | async-start | bytes 1216512 | tf_op jit(solution)/shard_map/all_gather | solution.py:148
  7.9 115.7 %all-gather.9.cloned.1.call-start = ((), (), s32[]{:S(2)}) async-start(), calls=%async_computation.7 | async-start | bytes 1216512 | tf_op jit(solution)/shard_map/all_gather | solution.py:149
  8.7 170.7 %all-gather.11.cloned.1.call-start = ((), (), s32[]{:S(2)}) async-start(), calls=%async_computation.8 | async-start | bytes 1216512 | tf_op jit(solution)/shard_map/all_gather | solution.py:150
  9.4 225.5 %all-gather.13.cloned.1.call-start = ((), (), s32[]{:S(2)}) async-start(), calls=%async_computation.9 | async-start | bytes 1216512 | tf_op jit(solution)/shard_map/all_gather | solution.py:151
  10.0 290.2 %all-gather.15.cloned.1.call-start = ((), (), s32[]{:S(2)}) async-start(), calls=%async_computation.10 | async-start | bytes 4866048 | tf_op jit(solution)/shard_map/all_gather | solution.py:198
  10.6 354.4 %all-gather.17.cloned.1.call-start = ((), (), s32[]{:S(2)}) async-start(), calls=%async_computation.11 | async-start | bytes 4866048 | tf_op jit(solution)/shard_map/all_gather | solution.py:199
  11.2 750.4 %reduce-scatter.13.cloned.1.call-start = ((), (), s32[]{:S(2)}) async-start(), calls=%async_computation.12 | async-start | bytes 2433024 | tf_op jit(solution)/shard_map/reduce_scatter | solution.py:279
  15.9 110.9 %copy-start.162 = (f32[64]{0:T(128)}, f32[64]{0:T(128)S(1)}, u32[]{:S(2)}) copy-start(f32[64]{0:T(128)S(1)} %subtract_convert_fusion) | copy-start | bytes 772
  15.9 110.9 %copy-start.165 = (s32[64]{0:T(128)}, s32[64]{0:T(128)S(1)}, u32[]{:S(2)}) copy-start(s32[64]{0:T(128)S(1)} %get-tuple-element.279) | copy-start | bytes 772
  15.9 110.9 %copy-start.168 = (s32[64]{0:T(128)}, s32[64]{0:T(128)S(1)}, u32[]{:S(2)}) copy-start(s32[64]{0:T(128)S(1)} %get-tuple-element.280) | copy-start | bytes 772
  79.5 51.6 %copy-start.2 = (f32[1024,768]{0,1:T(8,128)}, f32[1024,768]{0,1:T(8,128)S(1)}, u32[]{:S(2)}) copy-start(f32[1024,768]{0,1:T(8,128)S(1)} %add_multiply_fusion.3) | copy-start | bytes 9437188
  82.2 54.2 %copy-start.29 = (f32[12,64,64]{2,1,0:T(8,128)}, f32[12,64,64]{2,1,0:T(8,128)S(1)}, u32[]{:S(2)}) copy-start(f32[12,64,64]{2,1,0:T(8,128)S(1)} %fusion.113) | copy-start | bytes 589828
  238.8 165.9 %copy-start.28 = (f32[1024,768]{0,1:T(8,128)}, f32[1024,768]{0,1:T(8,128)S(1)}, u32[]{:S(2)}) copy-start(f32[1024,768]{0,1:T(8,128)S(1)} %get-tuple-element.260) | copy-start | bytes 9437188
  454.1 307.5 %reduce-scatter.19.cloned.1.call-start = ((), (), s32[]{:S(2)}) async-start(), calls=%async_computation.15 | async-start | bytes 2433024
  520.2 241.3 %reduce-scatter.21.cloned.1.call-start = ((), (), s32[]{:S(2)}) async-start(), calls=%async_computation.16 | async-start | bytes 2433024
  554.4 311.1 %reduce-scatter.23.cloned.1.call-start = ((), (), s32[]{:S(2)}) async-start(), calls=%async_computation.17 | async-start | bytes 2433024
  554.5 35.0 %copy-start.85 = (f32[12,64,64]{2,1,0:T(8,128)S(1)}, f32[12,64,64]{2,1,0:T(8,128)}, u32[]{:S(2)}) copy-start(f32[12,64,64]{2,1,0:T(8,128)} %fusion.186) | copy-start | bytes 589828
  554.5 35.0 %copy-start.125 = (f32[12,64]{1,0:T(8,128)S(1)}, f32[12,64]{1,0:T(8,128)}, u32[]{:S(2)}) copy-start(f32[12,64]{1,0:T(8,128)} %copy-done.122) | copy-start | bytes 9220
  554.5 35.0 %copy-start.129 = (f32[1024]{0:T(1024)S(1)}, f32[1024]{0:T(1024)}, u32[]{:S(2)}) copy-start(f32[1024]{0:T(1024)} %add_multiply_fusion.4) | copy-start | bytes 12292
  642.5 364.7 %reduce-scatter.15.cloned.1.call-start = ((), (), s32[]{:S(2)}) async-start(), calls=%async_computation.13 | async-start | bytes 9732096 | tf_op jit(solution)/shard_map/reduce_scatter | solution.py:233
  653.1 495.5 %reduce-scatter.17.cloned.1.call-start = ((), (), s32[]{:S(2)}) async-start(), calls=%async_computation.14 | async-start | bytes 9732096 | tf_op jit(solution)/shard_map/reduce_scatter | solution.py:234
  680.8 33.5 %copy-start.151 = (f32[768]{0:T(1024)S(1)}, f32[768]{0:T(1024)}, u32[]{:S(2)}) copy-start(f32[768]{0:T(1024)} %get-tuple-element.191) | copy-start | bytes 9220
  680.8 33.5 %copy-start.153 = (f32[768]{0:T(1024)S(1)}, f32[768]{0:T(1024)}, u32[]{:S(2)}) copy-start(f32[768]{0:T(1024)} %get-tuple-element.129) | copy-start | bytes 9220
  (260 other events, 1948.8 us)
Sparse Core Ops, SparseCore 0:
  10.9 56.8 all-gather.6
  70.7 52.8 all-gather.8
  126.5 52.8 all-gather.10
  182.1 52.8 all-gather.12
  237.7 62.4 all-gather.14
  303.0 61.9 all-gather.16
  454.2 97.9 reduce-scatter.12
  558.0 98.5 reduce-scatter.18
  662.5 98.7 reduce-scatter.20
  766.9 98.4 reduce-scatter.22
  872.0 135.2 reduce-scatter.14
  1013.6 135.0 reduce-scatter.16
where the time goes:
time: 1160 us
  waiting for transfers between devices  575 us (50%)
  matrix products  290 us (25%)
  other arithmetic  135 us (12%)
  blocking collectives  83.1 us (7%)
  local copies, waits for them, and re-layouts  53 us (5%)
  between operations  19.4 us (2%)
    dot_general x94, matrix products, batch_mapped(): jnp.einsum(form, left, right, precision=lax.Precision.HIGHEST, preferred_...  189 us
    reduce_scatter x1, waiting for transfers between devices, on_device(): lax.psum_scatter(up_weight_grad, ('wide', 'narrow'), scatter_dimension=0,...  142 us
    reduce_scatter x1, waiting for transfers between devices, on_device(): lax.psum_scatter(down_weight_grad, ('wide', 'narrow'), scatter_dimension=...  141 us
    unnamed x15, waiting for transfers between devices  108 us
    unnamed x2, blocking collectives  83.1 us
    all_gather x1, waiting for transfers between devices, on_device(): lax.all_gather(up_weight, ('wide', 'narrow'), axis=0, tiled=True)  57.2 us
    all_gather x1, waiting for transfers between devices, on_device(): lax.all_gather(down_weight, ('wide', 'narrow'), axis=0, tiled=True)  52.1 us
    unnamed x579, local copies, waits for them, and re-layouts  50.7 us
  transfers between devices with their start and end apart: 12, of which 8 were waited for; matrix products, arithmetic and copies ran while one was open for 33% of the time, Pallas kernels for 0%

commit v1 on v0

--- a/solution.py
+++ b/solution.py
@@ -116,6 +116,10 @@
 
 def column_sums(rows):
     return jnp.sum(rows.astype(jnp.float32), axis=0)
+
+
+def pad_lanes(block):
+    return jnp.pad(block, ((0, 0), (0, 128 - block.shape[1])))
 
 
 def on_device(
@@ -144,28 +148,48 @@
     width = tokens.shape[1]
     devices = lax.axis_size(("wide", "narrow"))
     shaped = (seq_count, seq_len, width)
-    attention_full = (
-        lax.all_gather(query_weight, ("wide", "narrow"), axis=0, tiled=True),
-        lax.all_gather(key_weight, ("wide", "narrow"), axis=0, tiled=True),
-        lax.all_gather(value_weight, ("wide", "narrow"), axis=0, tiled=True),
-        lax.all_gather(output_weight, ("wide", "narrow"), axis=0, tiled=True),
-        lax.all_gather(query_bias, ("wide", "narrow"), axis=0, tiled=True),
-        lax.all_gather(value_bias, ("wide", "narrow"), axis=0, tiled=True),
-        lax.all_gather(output_bias, ("wide", "narrow"), axis=0, tiled=True),
-        lax.all_gather(norm_gain, ("wide", "narrow"), axis=0, tiled=True),
-        lax.all_gather(norm_bias, ("wide", "narrow"), axis=0, tiled=True),
-    )
-    (
-        query_full,
-        key_full,
-        value_full,
-        output_full,
-        query_add,
-        value_add,
-        output_add,
-        gain_one,
-        shift_one,
-    ) = attention_full
+    axes = ("wide", "narrow")
+    units = query_bias.shape[0]
+    ratio = up_bias.shape[0] // units
+    hidden = up_weight.shape[1]
+    small_one = pad_lanes(
+        jnp.stack([query_bias, value_bias, output_bias, norm_gain, norm_bias], axis=1)
+    )
+    packed_one = jnp.concatenate(
+        [query_weight, key_weight, value_weight, output_weight, small_one], axis=1
+    )
+    up_mixed = up_weight.reshape(units, width, ratio).swapaxes(1, 2).reshape(units, hidden)
+    small_two = pad_lanes(
+        jnp.concatenate(
+            [
+                up_bias.reshape(units, ratio),
+                jnp.stack([down_bias, final_gain, final_bias], axis=1),
+            ],
+            axis=1,
+        )
+    )
+    packed_two = jnp.concatenate(
+        [up_mixed, down_weight.reshape(units, hidden), small_two], axis=1
+    )
+    full_one = lax.all_gather(packed_one, axes, axis=0, tiled=True)
+    full_two = lax.all_gather(packed_two, axes, axis=0, tiled=True)
+    query_full = full_one[:, :width]
+    key_full = full_one[:, width : 2 * width]
+    value_full = full_one[:, 2 * width : 3 * width]
+    output_full = full_one[:, 3 * width : 4 * width]
+    query_add, value_add, output_add, gain_one, shift_one = (
+        full_one[:, 4 * width + n] for n in range(5)
+    )
+    up_full = full_two[:, :hidden]
+    down_full = (
+        full_two[:, hidden : 2 * hidden]
+        .reshape(width, ratio, width)
+        .swapaxes(0, 1)
+        .reshape(hidden, width)
+    )
+    tail = full_two[:, 2 * hidden :]
+    up_add = tail[:, :ratio].T.reshape(hidden)
+    down_add, gain_two, shift_two = (tail[:, ratio + n] for n in range(3))
     queries = matmul(tokens, query_full) + query_add.astype(jnp.float32)
     keys = matmul(tokens, key_full)
     values = matmul(tokens, value_full) + value_add.astype(jnp.float32)
@@ -194,15 +218,6 @@
         layer_norm, first_sum, gain_one.astype(jnp.float32), shift_one.astype(jnp.float32)
     )
     hidden_low = first_norm.astype(jnp.bfloat16)
-    feed_full = (
-        lax.all_gather(up_weight, ("wide", "narrow"), axis=0, tiled=True),
-        lax.all_gather(down_weight, ("wide", "narrow"), axis=0, tiled=True),
-        lax.all_gather(up_bias, ("wide", "narrow"), axis=0, tiled=True),
-        lax.all_gather(down_bias, ("wide", "narrow"), axis=0, tiled=True),
-        lax.all_gather(final_gain, ("wide", "narrow"), axis=0, tiled=True),
-        lax.all_gather(final_bias, ("wide", "narrow"), axis=0, tiled=True),
-    )
-    up_full, down_full, up_add, down_add, gain_two, shift_two = feed_full
     up_rows = matmul(hidden_low, up_full) + up_add.astype(jnp.float32)
     activated, gelu_back = jax.vjp(gelu_exact, up_rows)
     activated_low = activated.astype(jnp.bfloat16)
@@ -210,16 +225,8 @@
     result, final_back = jax.vjp(
         layer_norm, second_sum, gain_two.astype(jnp.float32), shift_two.astype(jnp.float32)
     )
-    feed_again = (
-        lax.all_gather(up_weight, ("wide", "narrow"), axis=0, tiled=True),
-        lax.all_gather(down_weight, ("wide", "narrow"), axis=0, tiled=True),
-        lax.all_gather(up_bias, ("wide", "narrow"), axis=0, tiled=True),
-        lax.all_gather(down_bias, ("wide", "narrow"), axis=0, tiled=True),
-        lax.all_gather(final_gain, ("wide", "narrow"), axis=0, tiled=True),
-        lax.all_gather(final_bias, ("wide", "narrow"), axis=0, tiled=True),
-    )
-    up_back = feed_again[0]
-    down_back = feed_again[1]
+    up_back = up_full
+    down_back = down_full
     second_grad, final_gain_grad, final_bias_grad = final_back(cotangent.astype(jnp.float32))
     down_in = second_grad.astype(jnp.bfloat16)
     down_weight_grad = matmul_left_t(activated_low, down_in)
@@ -229,29 +236,18 @@
     up_weight_grad = matmul_left_t(hidden_low, up_in)
     up_bias_grad = column_sums(up_in)
     hidden_grad = second_grad + matmul_right_t(up_in, up_back)
-    feed_owned = (
-        lax.psum_scatter(up_weight_grad, ("wide", "narrow"), scatter_dimension=0, tiled=True),
-        lax.psum_scatter(down_weight_grad, ("wide", "narrow"), scatter_dimension=0, tiled=True),
-        lax.psum_scatter(up_bias_grad, ("wide", "narrow"), scatter_dimension=0, tiled=True),
-        lax.psum_scatter(down_bias_grad, ("wide", "narrow"), scatter_dimension=0, tiled=True),
-        lax.psum_scatter(final_gain_grad, ("wide", "narrow"), scatter_dimension=0, tiled=True),
-        lax.psum_scatter(final_bias_grad, ("wide", "narrow"), scatter_dimension=0, tiled=True),
-    )
-    attention_again = (
-        lax.all_gather(query_weight, ("wide", "narrow"), axis=0, tiled=True),
-        lax.all_gather(key_weight, ("wide", "narrow"), axis=0, tiled=True),
-        lax.all_gather(value_weight, ("wide", "narrow"), axis=0, tiled=True),
-        lax.all_gather(output_weight, ("wide", "narrow"), axis=0, tiled=True),
-        lax.all_gather(query_bias, ("wide", "narrow"), axis=0, tiled=True),
-        lax.all_gather(value_bias, ("wide", "narrow"), axis=0, tiled=True),
-        lax.all_gather(output_bias, ("wide", "narrow"), axis=0, tiled=True),
-        lax.all_gather(norm_gain, ("wide", "narrow"), axis=0, tiled=True),
-        lax.all_gather(norm_bias, ("wide", "narrow"), axis=0, tiled=True),
-    )
-    query_back = attention_again[0]
-    key_back = attention_again[1]
-    value_back = attention_again[2]
-    output_back = attention_again[3]
+    down_mixed = (
+        down_weight_grad.reshape(ratio, width, width).swapaxes(0, 1).reshape(width, hidden)
+    )
+    feed_owned = lax.psum_scatter(
+        jnp.concatenate([up_weight_grad, down_mixed], axis=1).astype(jnp.bfloat16),
+        axes,
+        scatter_dimension=0,
+        tiled=True,
+    ).astype(jnp.float32)
+    up_owned = feed_owned[:, :hidden].reshape(units, ratio, width).swapaxes(1, 2)
+    down_owned = feed_owned[:, hidden:].reshape(units * ratio, width)
+    query_back, key_back, value_back, output_back = query_full, key_full, value_full, output_full
     first_grad, norm_gain_grad, norm_bias_grad = norm_back(hidden_grad)
     attend_in = first_grad.astype(jnp.bfloat16)
     output_weight_grad = matmul_left_t(context_low, attend_in)
@@ -272,38 +268,52 @@
         + matmul_right_t(key_in, key_back)
         + matmul_right_t(value_in, value_back)
     )
-    attention_owned = (
-        lax.psum_scatter(query_weight_grad, ("wide", "narrow"), scatter_dimension=0, tiled=True),
-        lax.psum_scatter(key_weight_grad, ("wide", "narrow"), scatter_dimension=0, tiled=True),
-        lax.psum_scatter(value_weight_grad, ("wide", "narrow"), scatter_dimension=0, tiled=True),
-        lax.psum_scatter(output_weight_grad, ("wide", "narrow"), scatter_dimension=0, tiled=True),
-        lax.psum_scatter(query_bias_grad, ("wide", "narrow"), scatter_dimension=0, tiled=True),
-        lax.psum_scatter(value_bias_grad, ("wide", "narrow"), scatter_dimension=0, tiled=True),
-        lax.psum_scatter(output_bias_grad, ("wide", "narrow"), scatter_dimension=0, tiled=True),
-        lax.psum_scatter(norm_gain_grad, ("wide", "narrow"), scatter_dimension=0, tiled=True),
-        lax.psum_scatter(norm_bias_grad, ("wide", "narrow"), scatter_dimension=0, tiled=True),
-    )
-    proxy_total, conv_total = lax.psum((jnp.sum(proxies, axis=0), conv_grad), ("wide", "narrow"))
+    attention_owned = lax.psum_scatter(
+        jnp.concatenate(
+            [query_weight_grad, key_weight_grad, value_weight_grad, output_weight_grad], axis=1
+        ).astype(jnp.bfloat16),
+        axes,
+        scatter_dimension=0,
+        tiled=True,
+    ).astype(jnp.float32)
+    columns = jnp.stack(
+        [
+            query_bias_grad,
+            value_bias_grad,
+            output_bias_grad,
+            norm_gain_grad,
+            norm_bias_grad,
+            down_bias_grad,
+            final_gain_grad,
+            final_bias_grad,
+        ]
+    )
+    columns, up_bias_total, proxy_total, conv_total = lax.psum(
+        (columns, up_bias_grad.reshape(ratio, width), jnp.sum(proxies, axis=0), conv_grad), axes
+    )
+    own = lax.axis_index(axes) * units
+    columns = lax.dynamic_slice_in_dim(columns, own, units, axis=1)
+    up_bias_owned = lax.dynamic_slice_in_dim(up_bias_total, own, units, axis=1).T.reshape(-1)
     proxy = proxy_total / (seq_count * devices)
     return (
         result,
         tokens_grad,
-        attention_owned[0],
-        attention_owned[1],
-        attention_owned[2],
-        attention_owned[4],
-        attention_owned[5],
+        attention_owned[:, :width],
+        attention_owned[:, width : 2 * width],
+        attention_owned[:, 2 * width : 3 * width],
+        columns[0],
+        columns[1],
         conv_total,
-        attention_owned[3],
-        attention_owned[6],
-        attention_owned[7],
-        attention_owned[8],
-        feed_owned[0],
-        feed_owned[2],
-        feed_owned[1],
-        feed_owned[3],
-        feed_owned[4],
-        feed_owned[5],
+        attention_owned[:, 3 * width :],
+        columns[2],
+        columns[3],
+        columns[4],
+        up_owned.reshape(units, hidden),
+        up_bias_owned,
+        down_owned,
+        columns[5],
+        columns[6],
+        columns[7],
         proxy,
     )
 

time: 1160 us -> 758 us (0.65)
  waiting for transfers between devices: 575 us -> 169 us
  blocking collectives: 83.1 us -> 40.2 us
  local copies, waits for them, and re-layouts: 53 us -> 77.9 us
  other arithmetic: 135 us -> 148 us
    reduce_scatter x3 -> x1, waiting for transfers between devices: 283 us -> 118 us  [on_device(): lax.psum_scatter(jnp.concatenate([up_weight_grad, down_mixed], axis=1).as...]
    all_gather x6 -> x2, waiting for transfers between devices: 184 us -> 50.7 us  [the longest x1 50.7 us: on_device(): full_one = lax.all_gather(packed_one, axes, axis=0, tiled=True)]
    unnamed x15 -> x5, waiting for transfers between devices: 108 us -> 0.07 us
    unnamed x2 -> x0, blocking collectives: 83.1 us -> none
    psum x0 -> x1, blocking collectives: none -> 40.2 us  [on_device(): lax.psum((columns, up_bias_grad.reshape(ratio, width), jnp.sum(proxies, a...]
    slice x0 -> x4, local copies, waits for them, and re-layouts: none -> 12.5 us  [the longest x2 11.4 us: on_device(): full_two[:, hidden:2 * hidden].reshape(width, ratio, width).swapaxes(0, 1)]
    unnamed x579 -> x486, local copies, waits for them, and re-layouts: 50.7 us -> 41.3 us
  transfers between devices with their start and end apart: 12 -> 4, of which waited for: 8 -> 2; matrix products, arithmetic and copies ran while one was open for 33% -> 27% of each run, Pallas kernels for 0% -> 0%
where the time goes in v1:
time: 758 us; the launch traced here: 747 us
  matrix products  293 us (39%)
  waiting for transfers between devices  169 us (22%)
  other arithmetic  148 us (20%)
  local copies, waits for them, and re-layouts  77.9 us (10%)
  blocking collectives  40.2 us (5%)
  between operations  18.5 us (2%)
    dot_general x94, matrix products, batch_mapped(): jnp.einsum(form, left, right, precision=lax.Precision.HIGHEST, preferred_...  198 us
    reduce_scatter x1, waiting for transfers between devices, on_device(): lax.psum_scatter(jnp.concatenate([up_weight_grad, down_mixed], axis=1).as...  118 us
    all_gather x1, waiting for transfers between devices, on_device(): full_one = lax.all_gather(packed_one, axes, axis=0, tiled=True)  50.7 us
    unnamed x486, local copies, waits for them, and re-layouts  41.3 us
    psum x1, blocking collectives, on_device(): lax.psum((columns, up_bias_grad.reshape(ratio, width), jnp.sum(proxies, a...  40.2 us
    dot_general x6, matrix products, matmul_right_t(): lax.dot_general(left, right, (((1,), (1,)), ((), ())), preferred_element_...  40.1 us
    reduce_sum x3, other arithmetic, attention_core(): conv_weight[:, offset][None, :, None] * padded[offset:offset + seq_len]  39.4 us
    mul x2, other arithmetic, attention_core(): conv_weight[:, offset][None, :, None] * padded[offset:offset + seq_len]  35.5 us
  transfers between devices with their start and end apart: 4, of which 2 were waited for; matrix products, arithmetic and copies ran while one was open for 27% of the time, Pallas kernels for 0%

profile of v1, /device:TPU:0, one launch (start us, length us, event | category | flops | bytes accessed | tf_op | source)
XLA Modules:
  0.0 746.7 jit_solution(10060342198021636227)
XLA Ops:
  28.4 50.7 %all-gather.3.cloned.1.call-done = bf16[768,3200]{1,0:T(8,128)(2,1)} async-done(((bf16[24,3200]{1,0:T(8,128)(2,1)}), bf16[768,3200]{1,0:T(8,128)(2,1)}) %all-gather.3.cloned.1.call-update) | async-done | bytes 4915216 | tf_op jit(solution)/shard_map/all_gather | solution.py:174
  98.9 13.6 %fusion.210 = (f32[12,1024]{1,0:T(8,128)S(1)}, f32[12,1024,64]{1,2,0:T(8,128)S(1)}) fusion(f32[1024,12,64]{0,2,1:T(8,128)} %bitcast.631, f32[12,64,64]{2,1,0:T(8,128)S(1)} %fusion.132), kind=kOutput, calls=%fused_computation.514 | convolution fusion | flops 604753920 | bytes 6537216 | tf_op jit(solution)/shard_map/jvp(vmap(bsz,scz->sbc))/dot_general | solution.py:15
  144.7 29.2 %fusion.14 = bf16[1,1024,12,64]{1,3,2,0:T(8,128)(2,1)} fusion(f32[1,1024,12,64]{1,3,2,0:T(8,128)S(1)} %bitcast.634, f32[12,64,64]{2,1,0:T(8,128)S(1)} %fusion.213, f32[1024]{0:T(1024)S(1)} %copy-done.129, f32[12]{0:T(128)S(1)} %copy-done.186, f32[12]{0:T(128)S(1)} %copy-done.190, f32[12]{0:T(128)S(1)} %copy-done.191, f32[12]{0:T(128)S(1)} %copy-done.192, ...), kind=kOutput, calls=%fused_computation.37 | convolution fusion | flops 659030016 | bytes 8164912 | tf_op jit(solution)/shard_map/jvp(vmap(bqj,bjg->qbg))/dot_general | solution.py:15
  186.3 4.8 slice.427
  191.1 6.6 copy.367
  197.7 6.6 copy.368
  206.1 12.2 %multiply_convert_fusion = (bf16[1024,3072]{1,0:T(8,128)(2,1)S(1)}, f32[1024,3072]{1,0:T(8,128)}) fusion(f32[3072]{0:T(1024)} %reshape.2169, bf16[768,6272]{1,0:T(8,128)(2,1)} %all-gather.5.cloned.1.call-done, f32[1024,768]{0,1:T(8,128)S(1)} %get-tuple-element.285, f32[768]{0:T(1024)} %get-tuple-element.152, f32[768]{0:T(1024)} %get-tuple-element.151, ...), kind=kOutput, calls=%fused_computation.2 | convolution fusion | flops 4854644736 | bytes 26767360 | tf_op jit(solution)/shard_map/dot_general | solution.py:21
  218.4 5.8 fusion.212
  231.7 15.3 %convert_reduce_fusion = (f32[3072]{0:T(1024)}, bf16[1024,3072]{1,0:T(8,128)(2,1)S(1)}) fusion(bf16[1024,768]{0,1:T(8,128)(2,1)S(1)} %get-tuple-element.203, bf16[3072,768]{1,0:T(8,128)(2,1)S(1)} %bitcast.645, f32[1024,3072]{1,0:T(8,128)} %get-tuple-element.287, f32[3072]{0:T(1024)S(1)} %copy-done.155), kind=kOutput, calls=%fused_computation | convolution fusion | flops 4882166784 | bytes 25190400 | tf_op jit(solution)/shard_map/dot_general | solution.py:31
  247.1 11.4 %multiply_reduce_fusion.32 = (f32[768]{0:T(1024)}, f32[1024]{0:T(1024)S(1)}, f32[768]{0:T(1024)}, f32[1024,768]{0,1:T(8,128)S(1)}) fusion(f32[1024,768]{0,1:T(8,128)S(1)} %get-tuple-element.285, f32[1024]{0:T(1024)S(1)} %copy-done.151, f32[1024]{0:T(1024)S(1)} %copy-done.137, f32[768]{0:T(1024)S(1)} %copy-done.147, ...), kind=kOutput, calls=%fused_computation.79 | convolution fusion | flops 4845204480 | bytes 22061056 | tf_op jit(solution)/shard_map/dot_general | solution.py:31
  304.3 4.9 convert_reduce_fusion.7
  315.2 5.1 fusion.23
  330.6 5.1 fusion.24
  335.7 17.0 %broadcast_multiply_fusion.2 = (f32[1,1024,12,64]{1,3,2,0:T(8,128)}, f32[1,1024,12,64]{1,3,2,0:T(8,128)}, f32[1,1024,12,64]{1,3,2,0:T(8,128)}, f32[1,1024,12,64]...) fusion(f32[12]{0:T(128)} %get-tuple-element.166, ...), kind=kLoop, calls=%fused_computation.159 | loop fusion | flops 13369344 | bytes 53482240 | tf_op jit(solution)/shard_map/transpose(jvp(vmap()))/mul | solution.py:94
  352.7 18.4 %broadcast_multiply_fusion.1 = (f32[1,1024,12,64]{1,3,2,0:T(8,128)}, f32[1,1024,12,64]{1,3,2,0:T(8,128)}, f32[1,1024,12,64]{1,3,2,0:T(8,128)}, f32[1,1024,12,64]...) fusion(f32[12]{0:T(128)} %get-tuple-element.165, ...), kind=kLoop, calls=%fused_computation.158 | loop fusion | flops 14155776 | bytes 56628016 | tf_op jit(solution)/shard_map/transpose(jvp(vmap()))/mul | solution.py:94
  395.3 34.2 %pad_add_fusion = f32[1,1056,12,64]{1,3,2,0:T(8,128)} fusion(f32[1,1024,12,64]{1,3,2,0:T(8,128)} %get-tuple-element.231, f32[1,1024,12,64]{1,3,2,0:T(8,128)} %get-tuple-element.232, f32[1,1024,12,64]{1,3,2,0:T(8,128)} %get-tuple-element.233, f32[1,1024,12,64]{1,3,2,0:T(8,128)} %get-tuple-element.234, f32[1,1024,12,64]{1,3,2,0:T(8,128)} %get-tuple-element.235, ...), kind=kLoop, calls=%fused_computation.19 | loop fusion | flops 21086208 | bytes 88178688 | tf_op jit(solution)/shard_map/transpose(jvp(vmap()))/add_any | solution.py:94
  429.5 44.3 %multiply_reduce_fusion.30 = (f32[12]{0:T(128)}, f32[12]{0:T(128)}, f32[12]{0:T(128)}, f32[12]{0:T(128)}, f32[12]{0:T(128)}, /*index=5*/f32[12]{0:T(128)}, f32[1...) fusion(f32[1,1024,12,64]{1,3,2,0:T(8,128)} %bitcast.635, ...), kind=kOutput, calls=%fused_computation.76 | convolution fusion | flops 639368256 | bytes 34817744 | tf_op jit(solution)/shard_map/transpose(jvp(vmap(iob,bia->ioa)))/dot_general | solution.py:15
  482.6 6.6 copy.487
  489.3 8.2 %convolution_convert_fusion = bf16[3072,768]{1,0:T(8,128)(2,1)S(1)} fusion(bf16[1024,3072]{1,0:T(8,128)(2,1)} %copy-done.230, bf16[1024,768]{0,1:T(8,128)(2,1)} %copy-done.87), kind=kOutput, calls=%fused_computation.5 | convolution fusion | flops 4834197504 | bytes 12582912 | tf_op jit(solution)/shard_map/dot_general | solution.py:25
  503.1 8.5 %convolution_convert_fusion.1 = bf16[768,3072]{1,0:T(8,128)(2,1)S(1)} fusion(bf16[1024,3072]{1,0:T(8,128)(2,1)} %copy-done.229, f32[1024,768]{0,1:T(8,128)S(1)} %copy-done.27, f32[768]{0:T(1024)S(1)} %copy-done.166, f32[768]{0:T(1024)S(1)} %copy-done.148, f32[1024]{0:T(1024)S(1)} %copy-done.152, f32[1024]{0:T(1024)S(1)} %copy-done.138), kind=kOutput, calls=%fused_computation.6 | convolution fusion | flops 4838129664 | bytes 14170112 | tf_op jit(solution)/shard_map/dot_general | solution.py:25
  526.6 4.4 add_add_fusion.2
  535.1 35.6 %multiply_reduce_fusion.31 = (f32[12]{0:T(128)S(1)}, f32[12]{0:T(128)S(1)}, f32[12]{0:T(128)S(1)}, f32[12]{0:T(128)S(1)}, f32[12]{0:T(128)S(1)}, /*index=5*/f32[...) fusion(f32[1,1024,12,64]{1,3,2,0:T(8,128)} %bitcast.636, ...), kind=kLoop, calls=%fused_computation.77 | loop fusion | flops 27524916 | bytes 6296368 | tf_op jit(solution)/shard_map/transpose(jvp(vmap()))/reduce_sum | solution.py:94
  570.9 40.2 %all-reduce.69 = (f32[8,768]{1,0:T(8,128)S(1)}, f32[12,33]{0,1:T(8,128)S(1)}, f32[4,768]{1,0:T(4,128)S(1)}, f32[12]{0:T(128)S(1)}) all-reduce(f32[8,768]{1,0:T(8,128)S(1)} %stack.59, f32[12,33]{0,1:T(8,128)S(1)} %pad_add_fusion.7, f32[4,768]{1,0:T(4,128)S(1)} %reshape.2161, ...), channel_id=1, replica_groups=mesh['wide'=8,'narrow'=4] {'wide','narrow'}, use_global_device_ids=true, to_apply=%region_36.37 | all-reduce | flops 9624 | bytes 76992 | tf_op jit(solution)/shard_map/psum | solution.py:291
  618.2 118.0 %reduce-scatter.5.cloned.1.call-done = bf16[24,6144]{1,0:T(8,128)(2,1)} async-done(((bf16[768,6144]{1,0:T(8,128)(2,1)}), bf16[24,6144]{1,0:T(8,128)(2,1)}) %reduce-scatter.5.cloned.1.call-update) | async-done | bytes 294928 | tf_op jit(solution)/shard_map/reduce_scatter | solution.py:242
  (682 shorter events, 221.4 us)
Async XLA Ops:
  7.2 71.9 %all-gather.3.cloned.1.call-start = ((), (), s32[]{:S(2)}) async-start(), calls=%async_computation.2 | async-start | bytes 5068800 | tf_op jit(solution)/shard_map/all_gather | solution.py:174
  12.0 169.5 %all-gather.5.cloned.1.call-start = ((), (), s32[]{:S(2)}) async-start(), calls=%async_computation.3 | async-start | bytes 9934848 | tf_op jit(solution)/shard_map/all_gather | solution.py:175
  18.8 594.9 %reduce-scatter.7.cloned.1.call-start = ((), (), s32[]{:S(2)}) async-start(), calls=%async_computation.5 | async-start | bytes 4866048
  21.2 60.9 %copy-start.89 = (bf16[1024,768]{1,0:T(8,128)(2,1)S(1)}, bf16[1024,768]{1,0:T(8,128)(2,1)}, u32[]{:S(2)}) copy-start(bf16[1024,768]{1,0:T(8,128)(2,1)} %param.19) | copy-start | bytes 4718596
  23.9 66.7 %copy-start.156 = (f32[64]{0:T(128)}, f32[64]{0:T(128)S(1)}, u32[]{:S(2)}) copy-start(f32[64]{0:T(128)S(1)} %subtract_convert_fusion) | copy-start | bytes 772
  23.9 66.7 %copy-start.158 = (s32[64]{0:T(128)}, s32[64]{0:T(128)S(1)}, u32[]{:S(2)}) copy-start(s32[64]{0:T(128)S(1)} %get-tuple-element.304) | copy-start | bytes 772
  24.0 66.7 %copy-start.160 = (s32[64]{0:T(128)}, s32[64]{0:T(128)S(1)}, u32[]{:S(2)}) copy-start(s32[64]{0:T(128)S(1)} %get-tuple-element.305) | copy-start | bytes 772
  90.6 40.2 %copy-start.2 = (f32[768,1024]{1,0:T(8,128)}, f32[768,1024]{1,0:T(8,128)S(1)}, u32[]{:S(2)}) copy-start(f32[768,1024]{1,0:T(8,128)S(1)} %convolution_multiply_fusion) | copy-start | bytes 9437188
  134.6 45.7 %copy-start.133 = (f32[12,64]{1,0:T(8,128)}, f32[12,64]{1,0:T(8,128)S(1)}, u32[]{:S(2)}) copy-start(f32[12,64]{1,0:T(8,128)S(1)} %fusion.38) | copy-start | bytes 9220
  177.3 81.2 %copy-start.26 = (f32[1024,768]{0,1:T(8,128)}, f32[1024,768]{0,1:T(8,128)S(1)}, u32[]{:S(2)}) copy-start(f32[1024,768]{0,1:T(8,128)S(1)} %get-tuple-element.285) | copy-start | bytes 9437188
  272.2 48.1 %copy-start.83 = (f32[12,64,64]{2,1,0:T(8,128)}, f32[12,64,64]{2,1,0:T(8,128)S(1)}, u32[]{:S(2)}) copy-start(f32[12,64,64]{2,1,0:T(8,128)S(1)} %fusion.214) | copy-start | bytes 589828
  489.2 246.9 %reduce-scatter.5.cloned.1.call-start = ((), (), s32[]{:S(2)}) async-start(), calls=%async_computation.4 | async-start | bytes 9732096 | tf_op jit(solution)/shard_map/reduce_scatter | solution.py:242
  534.9 35.8 %copy-start.212 = (f32[12]{0:T(128)S(1)}, f32[12]{0:T(128)}, u32[]{:S(2)}) copy-start(f32[12]{0:T(128)} %get-tuple-element.134) | copy-start | bytes 148
  534.9 35.8 %copy-start.213 = (f32[12]{0:T(128)S(1)}, f32[12]{0:T(128)}, u32[]{:S(2)}) copy-start(f32[12]{0:T(128)} %get-tuple-element.135) | copy-start | bytes 148
  534.9 35.8 %copy-start.214 = (f32[12]{0:T(128)S(1)}, f32[12]{0:T(128)}, u32[]{:S(2)}) copy-start(f32[12]{0:T(128)} %get-tuple-element.136) | copy-start | bytes 148
  534.9 35.8 %copy-start.215 = (f32[12]{0:T(128)S(1)}, f32[12]{0:T(128)}, u32[]{:S(2)}) copy-start(f32[12]{0:T(128)} %get-tuple-element.137) | copy-start | bytes 148
  534.9 35.8 %copy-start.216 = (f32[12]{0:T(128)S(1)}, f32[12]{0:T(128)}, u32[]{:S(2)}) copy-start(f32[12]{0:T(128)} %get-tuple-element.138) | copy-start | bytes 148
  534.9 35.8 %copy-start.217 = (f32[12]{0:T(128)S(1)}, f32[12]{0:T(128)}, u32[]{:S(2)}) copy-start(f32[12]{0:T(128)} %get-tuple-element.139) | copy-start | bytes 148
  535.0 35.8 %copy-start.218 = (f32[12]{0:T(128)S(1)}, f32[12]{0:T(128)}, u32[]{:S(2)}) copy-start(f32[12]{0:T(128)} %get-tuple-element.140) | copy-start | bytes 148
  535.0 35.8 %copy-start.219 = (f32[12]{0:T(128)S(1)}, f32[12]{0:T(128)}, u32[]{:S(2)}) copy-start(f32[12]{0:T(128)} %get-tuple-element.141) | copy-start | bytes 148
  535.0 35.7 %copy-start.220 = (f32[12]{0:T(128)S(1)}, f32[12]{0:T(128)}, u32[]{:S(2)}) copy-start(f32[12]{0:T(128)} %get-tuple-element.142) | copy-start | bytes 148
  535.0 35.7 %copy-start.221 = (f32[12]{0:T(128)S(1)}, f32[12]{0:T(128)}, u32[]{:S(2)}) copy-start(f32[12]{0:T(128)} %get-tuple-element.143) | copy-start | bytes 148
  535.0 35.7 %copy-start.222 = (f32[12]{0:T(128)S(1)}, f32[12]{0:T(128)}, u32[]{:S(2)}) copy-start(f32[12]{0:T(128)} %get-tuple-element.144) | copy-start | bytes 148
  535.0 35.7 %copy-start.223 = (f32[12]{0:T(128)S(1)}, f32[12]{0:T(128)}, u32[]{:S(2)}) copy-start(f32[12]{0:T(128)} %get-tuple-element.145) | copy-start | bytes 148
  (213 other events, 1200.4 us)
Sparse Core Ops, SparseCore 0:
  12.1 66.9 all-gather.2
  82.1 80.5 all-gather.4
  489.4 105.7 reduce-scatter.6
  600.9 135.1 reduce-scatter.4

commit v2 on v1

--- a/solution.py
+++ b/solution.py
@@ -1,6 +1,8 @@
 import jax
 import jax.numpy as jnp
 from jax import lax
+from jax.experimental import pallas as pl
+from jax.experimental.pallas import tpu as pltpu
 from jax.sharding import PartitionSpec as P
 
 MARKS = 64
@@ -53,10 +55,8 @@
     return pseudo_inverse
 
 
-def attention_core(queries, keys, values, conv_weight, length):
+def attention_core(queries, keys, values, heads, length):
     seq_len = queries.shape[0]
-    heads = conv_weight.shape[0]
-    width = conv_weight.shape[1]
     head_dim = queries.shape[1] // heads
     scale = head_dim ** (-0.25)
     marks = MARKS
@@ -86,22 +86,127 @@
     pseudo_inverse = newton_inverse(second_kernel)
     mixed_output = batch_mapped("xkc,xcl->xkl", pseudo_inverse, landmark_value_rows)
     nystrom_attention = batch_mapped("bqj,bjg->qbg", first_kernel, mixed_output)
-    half = (width - 1) // 2
-    padded = jnp.pad(value_per_head, ((half, half), (0, 0), (0, 0)))
-    convolved = jnp.zeros_like(value_per_head)
-    for offset in range(width):
-        convolved = (
-            convolved + conv_weight[:, offset][None, :, None] * padded[offset : offset + seq_len]
-        )
-    context = ((nystrom_attention + convolved) * valid_mask[:, None, None]).reshape(
-        seq_len, heads * head_dim
-    )
+    context = (nystrom_attention * valid_mask[:, None, None]).reshape(seq_len, heads * head_dim)
     proxy = (
         jnp.sqrt(jnp.sum(second_kernel * second_kernel, axis=(1, 2)))
         * jnp.sqrt(jnp.sum(pseudo_inverse * pseudo_inverse, axis=(1, 2)))
         / marks
     )
     return (context, proxy)
+
+
+BLOCK = 128
+WINDOW = 256
+DEPTH = 64
+
+
+def banded(taps):
+    return pltpu.roll(
+        jnp.broadcast_to(taps, (BLOCK, WINDOW)), 0, 1, stride=1, stride_axis=0
+    )
+
+
+def fill_window(window_ref, rows, half):
+    span = rows.shape[0]
+    window_ref[:half] = jnp.zeros((half, rows.shape[1]), window_ref.dtype)
+    window_ref[half : half + span] = rows.astype(window_ref.dtype)
+    rest = window_ref.shape[0] - half - span
+    window_ref[half + span :] = jnp.zeros((rest, rows.shape[1]), window_ref.dtype)
+
+
+def banded_apply(taps_ref, window_refs, out_ref):
+    bands = jnp.concatenate([banded(taps_ref[0, 0:1]), banded(taps_ref[0, 1:2])], axis=0)
+    bands = bands.astype(jnp.bfloat16)
+    first = lax.broadcasted_iota(jnp.int32, (BLOCK, 2 * DEPTH), 1) < DEPTH
+    for block in range(out_ref.shape[0] // BLOCK):
+        both = sum(
+            matmul(bands, ref[block * BLOCK : block * BLOCK + WINDOW]) for ref in window_refs
+        )
+        out_ref[block * BLOCK : (block + 1) * BLOCK] = jnp.where(
+            first, both[:BLOCK], both[BLOCK:]
+        )
+
+
+def conv_kernel(half, taps_ref, rows_ref, out_ref, high_ref, low_ref):
+    rows = rows_ref[...]
+    high = rows.astype(jnp.bfloat16)
+    fill_window(high_ref, high, half)
+    fill_window(low_ref, rows - high.astype(jnp.float32), half)
+    banded_apply(taps_ref, (high_ref, low_ref), out_ref)
+
+
+def conv_back_kernel(half, taps_ref, rows_ref, grad_ref, out_ref, tap_grad_ref, rows_win, grad_win):
+    fill_window(rows_win, rows_ref[...], half)
+    fill_window(grad_win, grad_ref[...], half)
+    banded_apply(taps_ref, (grad_win,), out_ref)
+    first = lax.broadcasted_iota(jnp.int32, (BLOCK, 2 * DEPTH), 1) < DEPTH
+    total = jnp.zeros((2 * BLOCK, WINDOW), jnp.float32)
+    row = lax.broadcasted_iota(jnp.int32, (BLOCK, BLOCK), 0)
+    column = lax.broadcasted_iota(jnp.int32, (BLOCK, BLOCK), 1)
+    flip = (row + column == BLOCK - 1).astype(jnp.float32).astype(jnp.bfloat16)
+    for block in range(out_ref.shape[0] // BLOCK):
+        grad = matmul(
+            flip, grad_ref[block * BLOCK : (block + 1) * BLOCK].astype(jnp.bfloat16)
+        )
+        both = jnp.concatenate(
+            [jnp.where(first, grad, 0.0), jnp.where(first, 0.0, grad)], axis=0
+        ).astype(jnp.bfloat16)
+        total += matmul_right_t(both, rows_win[block * BLOCK : block * BLOCK + WINDOW])
+    for head in range(2):
+        turned = pltpu.roll(
+            total[head * BLOCK : (head + 1) * BLOCK],
+            0,
+            1,
+            stride=1,
+            stride_axis=0,
+        )
+        tap_grad_ref[0, head : head + 1] = jnp.sum(turned, axis=0, keepdims=True)
+
+
+def conv_specs(rows):
+    pair = pl.BlockSpec((rows.shape[0], 2 * DEPTH), lambda p: (0, p))
+    taps = pl.BlockSpec((1, 2, WINDOW), lambda p: (p, 0, 0))
+    return pair, taps
+
+
+def window_scratch(rows):
+    return pltpu.VMEM((rows.shape[0] + WINDOW, 2 * DEPTH), jnp.bfloat16)
+
+
+def pair_taps(weight):
+    heads, count = weight.shape
+    return jnp.pad(weight, ((0, 0), (0, WINDOW - count))).reshape(heads // 2, 2, WINDOW)
+
+
+def conv_forward(rows, weight):
+    pair, taps = conv_specs(rows)
+    return pl.pallas_call(
+        lambda *refs: conv_kernel((weight.shape[1] - 1) // 2, *refs),
+        grid=(weight.shape[0] // 2,),
+        in_specs=[taps, pair],
+        out_specs=pair,
+        out_shape=jax.ShapeDtypeStruct(rows.shape, jnp.float32),
+        scratch_shapes=[window_scratch(rows)] * 2,
+        name="conv_forward",
+    )(pair_taps(weight), rows)
+
+
+def conv_backward(rows, grad, weight):
+    pair, taps = conv_specs(rows)
+    heads, count = weight.shape
+    rows_grad, tap_grad = pl.pallas_call(
+        lambda *refs: conv_back_kernel((count - 1) // 2, *refs),
+        grid=(heads // 2,),
+        in_specs=[taps, pair, pair],
+        out_specs=[pair, taps],
+        out_shape=[
+            jax.ShapeDtypeStruct(rows.shape, jnp.float32),
+            jax.ShapeDtypeStruct((heads // 2, 2, WINDOW), jnp.float32),
+        ],
+        scratch_shapes=[window_scratch(rows)] * 2,
+        name="conv_backward",
+    )(pair_taps(weight[:, ::-1]), rows, grad)
+    return rows_grad, tap_grad.reshape(heads, WINDOW)[:, BLOCK - 1 : BLOCK - 1 + count]
 
 
 def layer_norm(rows, gain, shift):
@@ -195,20 +300,24 @@
     values = matmul(tokens, value_full) + value_add.astype(jnp.float32)
     conv_float = conv_weight.astype(jnp.float32)
 
-    def core_batch(query_in, key_in, value_in, conv_in):
+    heads = conv_weight.shape[0]
+    live = (jnp.arange(seq_len, dtype=jnp.int32) < lengths[0]).astype(jnp.float32)[:, None]
+
+    def core_batch(query_in, key_in, value_in):
         return jax.vmap(attention_core, in_axes=(0, 0, 0, None, 0))(
-            query_in, key_in, value_in, conv_in, lengths
-        )
-
+            query_in, key_in, value_in, heads, lengths
+        )
+
+    masked = values * live
+    convolved = conv_forward(masked, conv_float)
     context, core_back, proxies = jax.vjp(
         core_batch,
         queries.reshape(shaped),
         keys.reshape(shaped),
         values.reshape(shaped),
-        conv_float,
         has_aux=True,
     )
-    context_low = context.reshape(tokens.shape).astype(jnp.bfloat16)
+    context_low = (context.reshape(tokens.shape) + convolved * live).astype(jnp.bfloat16)
     first_sum = (
         tokens.astype(jnp.float32)
         + matmul(context_low, output_full)
@@ -239,8 +348,10 @@
     down_mixed = (
         down_weight_grad.reshape(ratio, width, width).swapaxes(0, 1).reshape(width, hidden)
     )
+    feed_packed = jnp.concatenate([up_weight_grad, down_mixed], axis=1).astype(jnp.bfloat16)
+    feed_packed, hidden_grad = lax.optimization_barrier((feed_packed, hidden_grad))
     feed_owned = lax.psum_scatter(
-        jnp.concatenate([up_weight_grad, down_mixed], axis=1).astype(jnp.bfloat16),
+        feed_packed,
         axes,
         scatter_dimension=0,
         tiled=True,
@@ -252,8 +363,10 @@
     attend_in = first_grad.astype(jnp.bfloat16)
     output_weight_grad = matmul_left_t(context_low, attend_in)
     output_bias_grad = column_sums(attend_in)
-    context_grad = matmul_right_t(attend_in, output_back).reshape(shaped)
-    query_grad, key_grad, value_grad, conv_grad = core_back(context_grad)
+    context_grad = matmul_right_t(attend_in, output_back)
+    query_grad, key_grad, value_grad = core_back(context_grad.reshape(shaped))
+    masked_grad, conv_grad = conv_backward(masked, context_grad * live, conv_float)
+    value_grad = value_grad.reshape(tokens.shape) + masked_grad * live
     query_in = query_grad.reshape(tokens.shape).astype(jnp.bfloat16)
     key_in = key_grad.reshape(tokens.shape).astype(jnp.bfloat16)
     value_in = value_grad.reshape(tokens.shape).astype(jnp.bfloat16)

time: 758 us -> 675 us (0.89)
  other arithmetic: 148 us -> 49.7 us
  matrix products: 293 us -> 212 us
  waiting for transfers between devices: 169 us -> 238 us
  Pallas kernels: 0 us -> 18.6 us
  local copies, waits for them, and re-layouts: 77.9 us -> 93.2 us
    dot_general x94, matrix products: 198 us -> 122 us  [batch_mapped(): jnp.einsum(form, left, right, precision=lax.Precision.HIGHEST, preferred_...]
    unnamed x5, waiting for transfers between devices: 0.07 us -> 48.9 us
    reduce_sum x3 -> x0, other arithmetic: 39.4 us -> none  [attention_core(): conv_weight[:, offset][None, :, None] * padded[offset:offset + seq_len]]
    add_any x2 -> x0, other arithmetic: 34.2 us -> none  [the longest x1 34.2 us: attention_core(): padded[offset:offset + seq_len]]
    mul x2 -> x1, other arithmetic: 35.5 us -> 3.9 us  [on_device(): context_grad * live]
    pallas_call x0 -> x2, Pallas kernels: none -> 18.6 us  [the longest x1 11.1 us: conv_backward(): pl.pallas_call(lambda *refs: conv_back_kernel((count - 1) // 2, *refs), g...]
    reduce_scatter x1, waiting for transfers between devices: 118 us -> 136 us  [on_device(): lax.psum_scatter(feed_packed, axes, scatter_dimension=0, tiled=True)]
    reshape x0 -> x5, local copies, waits for them, and re-layouts: none -> 8.76 us  [the longest x1 3.92 us: attention_core(): (values * valid_mask[:, None]).reshape(seq_len, heads, head_dim)]
  transfers between devices with their start and end apart: 4 -> 4, of which waited for: 2 -> 3; matrix products, arithmetic and copies ran while one was open for 27% -> 16% of each run, Pallas kernels for 0% -> 1%
where the time goes in v2:
time: 675 us; the launch traced here: 670 us
  waiting for transfers between devices  238 us (35%)
  matrix products  212 us (31%)
  local copies, waits for them, and re-layouts  93.2 us (14%)
  other arithmetic  49.7 us (7%)
  blocking collectives  40.9 us (6%)
  Pallas kernels  18.6 us (3%)
  between operations  18.2 us (3%)
    reduce_scatter x1, waiting for transfers between devices, on_device(): lax.psum_scatter(feed_packed, axes, scatter_dimension=0, tiled=True)  136 us
    dot_general x94, matrix products, batch_mapped(): jnp.einsum(form, left, right, precision=lax.Precision.HIGHEST, preferred_...  122 us
    all_gather x1, waiting for transfers between devices, on_device(): full_one = lax.all_gather(packed_one, axes, axis=0, tiled=True)  52.2 us
    unnamed x5, waiting for transfers between devices  48.9 us
    unnamed x401, local copies, waits for them, and re-layouts  42.8 us
    psum x1, blocking collectives, on_device(): lax.psum((columns, up_bias_grad.reshape(ratio, width), jnp.sum(proxies, a...  40.9 us
    dot_general x6, matrix products, matmul_right_t(): lax.dot_general(left, right, (((1,), (1,)), ((), ())), preferred_element_...  36.2 us
    dot_general x6, matrix products, matmul(): return jnp.dot(left, right, preferred_element_type=jnp.float32)  35 us
  transfers between devices with their start and end apart: 4, of which 3 were waited for; matrix products, arithmetic and copies ran while one was open for 16% of the time, Pallas kernels for 1%

profile of v2, /device:TPU:0, one launch (start us, length us, event | category | flops | bytes accessed | tf_op | source)
XLA Modules:
  0.0 670.1 jit_solution(288673852643193636)
XLA Ops:
  27.0 52.2 %all-gather.3.cloned.1.call-done = bf16[768,3200]{1,0:T(8,128)(2,1)} async-done(((bf16[24,3200]{1,0:T(8,128)(2,1)}), bf16[768,3200]{1,0:T(8,128)(2,1)}) %all-gather.3.cloned.1.call-update) | async-done | bytes 4915216 | tf_op jit(solution)/shard_map/all_gather | solution.py:279
  137.6 4.9 bitcast_multiply_fusion
  146.1 7.6 %conv_forward.1 = f32[1024,768]{1,0:T(8,128)} custom-call(f32[6,2,256]{2,1,0:T(2,128)} %reshape.1441.refs_0_, f32[1024,768]{1,0:T(8,128)} %copy-done.11), custom_call_target="tpu_custom_call" | custom-call | tf_op jit(solution)/shard_map/conv_forward/pallas_call | solution.py:183
  172.5 4.8 slice.136
  177.4 6.7 copy.387
  184.0 6.6 copy.388
  192.5 14.3 %multiply_convert_fusion = (bf16[1024,3072]{1,0:T(8,128)(2,1)}, f32[1024,3072]{1,0:T(8,128)}) fusion(f32[3072]{0:T(1024)} %reshape.1494, bf16[768,6272]{1,0:T(8,128)(2,1)} %all-gather.5.cloned.1.call-done, f32[1024,768]{0,1:T(8,128)} %copy-done.8, f32[768]{0:T(1024)} %get-tuple-element.128, f32[768]{0:T(1024)} %get-tuple-element.127, f32[1024]{0:T(1024)} %fusion.166, ...), kind=kOutput, calls=%fused_computation.2 | convolution fusion | flops 4854644736 | bytes 26767360 | tf_op jit(solution)/shard_map/dot_general | solution.py:23
  206.8 7.8 %fusion.212 = (f32[1024]{0:T(1024)S(1)}, f32[1024,768]{0,1:T(8,128)S(1)}) fusion(f32[768]{0:T(1024)S(1)} %get-tuple-element.124, bf16[1024,3072]{1,0:T(8,128)(2,1)} %get-tuple-element.195, bf16[3072,768]{1,0:T(8,128)(2,1)S(1)} %bitcast.593, f32[768]{0:T(1024)S(1)} %copy-done.176, f32[768]{0:T(1024)S(1)} %copy-done.147, f32[1024]{0:T(1024)S(1)} %copy-done.151, ...), kind=kOutput, calls=%fused_computation.377 | convolution fusion | flops 4837342208 | bytes 17323008 | tf_op jit(solution)/shard_map/dot_general | solution.py:23
  222.2 5.7 convolution_convert_fusion
  232.6 13.1 %convert_reduce_fusion = (f32[3072]{0:T(1024)}, bf16[1024,3072]{1,0:T(8,128)(2,1)S(1)}) fusion(bf16[1024,768]{0,1:T(8,128)(2,1)S(1)} %get-tuple-element.145, bf16[3072,768]{1,0:T(8,128)(2,1)} %bitcast.590, f32[1024,3072]{1,0:T(8,128)} %get-tuple-element.196, f32[3072]{0:T(1024)S(1)} %copy-done.167), kind=kOutput, calls=%fused_computation | convolution fusion | flops 4882166784 | bytes 25190400 | tf_op jit(solution)/shard_map/dot_general | solution.py:33
  245.8 6.0 convolution_convert_fusion.1
  255.8 9.9 %add_add_fusion.5 = f32[1024,768]{0,1:T(8,128)S(1)} fusion(bf16[1024,3072]{1,0:T(8,128)(2,1)} %copy-done.186, bf16[768,6272]{1,0:T(8,128)(2,1)} %all-gather.5.cloned.1.call-done, f32[1024]{0:T(1024)} %copy-done.158, f32[1024]{0:T(1024)} %copy-done.145, f32[1024,768]{0,1:T(8,128)} %copy-done.5, f32[1024]{0:T(1024)} %copy-done.140, f32[1024]{0:T(1024)} %copy-done.146, ...), kind=kOutput, calls=%fused_computation.62 | convolution fusion | flops 4838916096 | bytes 18894848 | tf_op jit(solution)/shard_map/dot_general | solution.py:33
  272.0 4.3 fusion.98
  280.1 6.5 fusion.12
  320.4 4.9 fusion.111
  325.3 4.3 convert_reduce_fusion.6
  331.5 4.1 fusion.22
  335.7 5.1 fusion.21
  340.8 4.4 convert_reduce_fusion.7
  374.6 11.1 %conv_backward.1 = (f32[1024,768]{1,0:T(8,128)}, f32[6,2,256]{2,1,0:T(2,128)}) custom-call(f32[6,2,256]{2,1,0:T(2,128)} %reshape.1478.refs_0_, f32[1024,768]{1,0:T(8,128)} %copy-done.11, f32[1024,768]{1,0:T(8,128)} %broadcast_multiply_fusion.refs_2_), custom_call_target="tpu_custom_call" | custom-call | tf_op jit(solution)/shard_map/conv_backward/pallas_call | solution.py:197
  404.4 6.7 copy.509
  427.3 40.9 %all-reduce.4 = (f32[8,768]{1,0:T(8,128)S(1)}, f32[12,33]{1,0:T(8,128)}, f32[4,768]{1,0:T(4,128)S(1)}, f32[12]{0:T(128)S(1)}) all-reduce(f32[8,768]{1,0:T(8,128)S(1)} %stack.59, f32[12,33]{1,0:T(8,128)S(1)} %slice.143, f32[4,768]{1,0:T(4,128)S(1)} %reshape.1486, ...), channel_id=1, replica_groups=mesh['wide'=8,'narrow'=4] {'wide','narrow'}, use_global_device_ids=true, to_apply=%region_36.37 | all-reduce | flops 9624 | bytes 76992 | tf_op jit(solution)/shard_map/psum | solution.py:404
  470.1 48.3 %reduce-scatter.7.cloned.1.call-done = bf16[24,3072]{1,0:T(8,128)(2,1)} async-done(((bf16[768,3072]{1,0:T(8,128)(2,1)}), bf16[24,3072]{1,0:T(8,128)(2,1)}) %reduce-scatter.7.cloned.1.call-update) | async-done | bytes 147472
  523.0 136.5 %reduce-scatter.5.cloned.1.call-done = bf16[24,6144]{1,0:T(8,128)(2,1)} async-done(((bf16[768,6144]{1,0:T(8,128)(2,1)}), bf16[24,6144]{1,0:T(8,128)(2,1)}) %reduce-scatter.5.cloned.1.call-update) | async-done | bytes 294928 | tf_op jit(solution)/shard_map/reduce_scatter | solution.py:353
  (604 shorter events, 235.3 us)
Async XLA Ops:
  7.2 11.6 %copy-start.91 = (bf16[1024,768]{1,0:T(8,128)(2,1)S(1)}, bf16[1024,768]{1,0:T(8,128)(2,1)}, u32[]{:S(2)}) copy-start(bf16[1024,768]{1,0:T(8,128)(2,1)} %param.37) | copy-start | bytes 4718596
  7.2 71.9 %all-gather.3.cloned.1.call-start = ((), (), s32[]{:S(2)}) async-start(), calls=%async_computation.2 | async-start | bytes 5068800 | tf_op jit(solution)/shard_map/all_gather | solution.py:279
  12.0 155.8 %all-gather.5.cloned.1.call-start = ((), (), s32[]{:S(2)}) async-start(), calls=%async_computation.3 | async-start | bytes 9934848 | tf_op jit(solution)/shard_map/all_gather | solution.py:280
  18.8 499.7 %reduce-scatter.7.cloned.1.call-start = ((), (), s32[]{:S(2)}) async-start(), calls=%async_computation.5 | async-start | bytes 4866048
  25.0 72.2 %copy-start.168 = (f32[64]{0:T(128)}, f32[64]{0:T(128)S(1)}, u32[]{:S(2)}) copy-start(f32[64]{0:T(128)S(1)} %subtract_convert_fusion) | copy-start | bytes 772
  25.1 72.1 %copy-start.170 = (s32[64]{0:T(128)}, s32[64]{0:T(128)S(1)}, u32[]{:S(2)}) copy-start(s32[64]{0:T(128)S(1)} %get-tuple-element.211) | copy-start | bytes 772
  25.1 72.1 %copy-start.172 = (s32[64]{0:T(128)}, s32[64]{0:T(128)S(1)}, u32[]{:S(2)}) copy-start(s32[64]{0:T(128)S(1)} %get-tuple-element.212) | copy-start | bytes 772
  25.1 59.8 %copy-start.136 = (f32[1024]{0:T(1024)}, f32[1024]{0:T(1024)S(1)}, u32[]{:S(2)}) copy-start(f32[1024]{0:T(1024)S(1)} %fusion.165) | copy-start | bytes 12292
  91.6 14.3 %copy-start = (f32[768,1024]{1,0:T(8,128)}, f32[768,1024]{1,0:T(8,128)S(1)}, u32[]{:S(2)}) copy-start(f32[768,1024]{1,0:T(8,128)S(1)} %add_multiply_fusion.2) | copy-start | bytes 9437188
  109.1 28.5 %copy-start.6 = (f32[12,1024,64]{1,2,0:T(8,128)}, f32[12,1024,64]{1,2,0:T(8,128)S(1)}, u32[]{:S(2)}) copy-start(f32[12,1024,64]{1,2,0:T(8,128)S(1)} %get-tuple-element.192) | copy-start | bytes 9437188
  109.1 28.5 %copy-start.119 = (f32[12,1024]{1,0:T(8,128)}, f32[12,1024]{1,0:T(8,128)S(1)}, u32[]{:S(2)}) copy-start(f32[12,1024]{1,0:T(8,128)S(1)} %get-tuple-element.191) | copy-start | bytes 147460
  110.4 27.2 %copy-start.121 = (f32[12,1024]{1,0:T(8,128)}, f32[12,1024]{1,0:T(8,128)S(1)}, u32[]{:S(2)}) copy-start(f32[12,1024]{1,0:T(8,128)S(1)} %fusion.24) | copy-start | bytes 147460
  190.7 16.1 %slice-start = ((s8[4718592]{0:T(1024)(128)(4,1)}), s8[4194304]{0:T(1024)(128)(4,1)S(1)}, s32[]{:S(2)}) async-start(s8[4718592]{0:T(1024)(128)(4,1)} %bitcast.591), calls=%async_computation.6 | async-start | bytes 8388608
  192.4 26.2 %copy-start.135 = (f32[768]{0:T(1024)}, f32[768]{0:T(1024)S(1)}, u32[]{:S(2)}) copy-start(f32[768]{0:T(1024)S(1)} %get-tuple-element.122) | copy-start | bytes 9220
  192.4 14.4 %copy-start.9 = (f32[1024,768]{0,1:T(8,128)S(1)}, f32[1024,768]{0,1:T(8,128)}, u32[]{:S(2)}) copy-start(f32[1024,768]{0,1:T(8,128)} %copy-done.8) | copy-start | bytes 9437188
  192.4 14.3 %slice-start.1 = ((s8[4718592]{0:T(1024)(128)(4,1)}), s8[524288]{0:T(1024)(128)(4,1)S(1)}, s32[]{:S(2)}) async-start(s8[4718592]{0:T(1024)(128)(4,1)} %bitcast.591), calls=%async_computation.7 | async-start | bytes 1048576
  192.4 14.3 %copy-start.142 = (f32[1024]{0:T(1024)S(1)}, f32[1024]{0:T(1024)}, u32[]{:S(2)}) copy-start(f32[1024]{0:T(1024)} %copy-done.141) | copy-start | bytes 12292
  192.4 14.3 %copy-start.147 = (f32[768]{0:T(1024)S(1)}, f32[768]{0:T(1024)}, u32[]{:S(2)}) copy-start(f32[768]{0:T(1024)} %get-tuple-element.127) | copy-start | bytes 9220
  192.4 14.3 %copy-start.151 = (f32[1024]{0:T(1024)S(1)}, f32[1024]{0:T(1024)}, u32[]{:S(2)}) copy-start(f32[1024]{0:T(1024)} %fusion.166) | copy-start | bytes 12292
  192.4 14.3 %copy-start.176 = (f32[768]{0:T(1024)S(1)}, f32[768]{0:T(1024)}, u32[]{:S(2)}) copy-start(f32[768]{0:T(1024)} %get-tuple-element.128) | copy-start | bytes 9220
  255.8 9.9 %copy-start.148 = (f32[768]{0:T(1024)S(1)}, f32[768]{0:T(1024)}, u32[]{:S(2)}) copy-start(f32[768]{0:T(1024)} %get-tuple-element.127) | copy-start | bytes 9220
  255.8 9.9 %copy-start.152 = (f32[1024]{0:T(1024)S(1)}, f32[1024]{0:T(1024)}, u32[]{:S(2)}) copy-start(f32[1024]{0:T(1024)} %fusion.166) | copy-start | bytes 12292
  374.6 11.1 %copy-start.139 = (f32[1024]{0:T(1024)S(1)}, f32[1024]{0:T(1024)}, u32[]{:S(2)}) copy-start(f32[1024]{0:T(1024)} %copy-done.136) | copy-start | bytes 12292
  411.1 248.4 %reduce-scatter.5.cloned.1.call-start = ((), (), s32[]{:S(2)}) async-start(), calls=%async_computation.4 | async-start | bytes 9732096 | tf_op jit(solution)/shard_map/reduce_scatter | solution.py:353
  (171 other events, 582.1 us)
Sparse Core Ops, SparseCore 0:
  12.1 66.9 all-gather.2
  82.0 80.6 all-gather.4
  411.2 107.2 reduce-scatter.6
  524.2 135.1 reduce-scatter.4
